TPU v7x, 32 devices: a whole 2x2x4 slice. The times are simulated.
32 devices in a mesh: dp: 16 (over z, x, core), mp: 2 (over y).
Axes of the slice: x: 2, y: 2, z: 4, core: 2. Of those that a mesh axis runs over, the one named last changes fastest.
Arguments:
- tokens: bfloat16 [2560, 1024], P('dp', 'mp'), may hold values from -6 to 6
- slot_embed: bfloat16 [2560, 1024], P('dp', 'mp'), may hold values from -0.1875 to 0.1875
- price_units: int32 [2560], P('dp'), may hold values from 0 to 1535
- unassigned: int32 [2560], P('dp'), may hold values from 0 to 1, as said below
Outputs:
- new_prices: float32 [2560], P(('dp', 'mp'))
- margins: float32 [2560], P('dp')
- unassigned_count: int32 [], replicated
Inputs may be any that keep to these rules, and one draw needn't show every extreme that they name: At most 128 of the 160 tokens of each index of dp are unassigned, and some index of dp has exactly 128 in every draw.
All inputs are finite; a program needn't handle non-finite values.
Results may differ from a plain program's by a relative error of at most 0.0004.
Values may be sent and summed in bfloat16 or wider, within the bound.
A program may use at most 128 MiB of HBM per device.

v0:
```python
import jax
import jax.numpy as jnp
from jax import lax
from jax.sharding import PartitionSpec as P

BUSY = 128
unit_price = 1.0 / 512.0


def merged(x, axis, combine):
    everything = jax.tree.map(lambda part: lax.all_gather(part, axis), x)
    first = jax.tree.map(lambda part: part[0], everything)

    def turn(k, so_far):
        return combine(so_far, jax.tree.map(lambda part: part[k], everything))

    return lax.fori_loop(1, lax.axis_size(axis), turn, first)


def top_two(values):
    best_value = jnp.max(values, axis=1)
    where_best = jnp.argmax(values, axis=1)
    column_ids = lax.broadcasted_iota(jnp.int32, values.shape, 1)
    second_value = jnp.max(jnp.where(column_ids == where_best[:, None], -jnp.inf, values), axis=1)
    return (best_value, second_value)


def keep_two(first, later):
    best_first, second_first = first
    best_later, second_later = later
    best_value = jnp.maximum(best_first, best_later)
    second_value = jnp.maximum(
        jnp.minimum(best_first, best_later), jnp.maximum(second_first, second_later)
    )
    return (best_value, second_value)


def compact(mask, busy):
    length = mask.shape[0]
    positions = lax.broadcasted_iota(jnp.int32, (length,), 0)
    ordering = jnp.argsort(jnp.where(mask > 0, positions, positions + length))[:busy]
    return (ordering, mask[ordering] > 0)


def spread_back(ordering, is_valid, margin_rows, length):
    positions = lax.broadcasted_iota(jnp.int32, (ordering.shape[0], length), 1)
    hits = (positions == ordering[:, None]) & is_valid[:, None]
    return jnp.sum(jnp.where(hits, margin_rows[:, None], jnp.float32(0.0)), axis=0)


def excess_of(values, second_value, is_valid):
    excess = jnp.where(is_valid[:, None], values - second_value[:, None], -jnp.inf)
    return jnp.max(excess, axis=0)


def on_device(tokens, slot_embed, price_units, unassigned):
    dp_count = lax.axis_size("dp")
    mp_count = lax.axis_size("mp")
    mp_index = lax.axis_index("mp")
    slot_dev = slot_embed.shape[0]
    half = slot_dev // mp_count
    columns = dp_count * half
    ordering, is_valid = compact(unassigned, BUSY)
    bidders = tokens[ordering]
    own_units = lax.dynamic_slice_in_dim(price_units, mp_index * half, half)
    own_prices = own_units.astype(jnp.float32) * unit_price
    whole_bidders = lax.all_gather(bidders, "mp", axis=1, tiled=True)
    slot_rows_whole = lax.all_to_all(slot_embed, "mp", split_axis=0, concat_axis=1, tiled=True)
    unit_all = jnp.zeros((columns,), jnp.int32)
    slot_rows = lax.all_gather(slot_rows_whole, "dp", axis=0, tiled=True)
    unit_rows = lax.all_gather(own_units, "dp", axis=0, tiled=True)
    block = jnp.einsum("bd,sd->bs", whole_bidders, slot_rows, preferred_element_type=jnp.float32)
    unit_all = lax.dynamic_update_slice_in_dim(unit_all, unit_rows, jnp.int32(0), 0)
    scores, unit_all = (block, unit_all)
    values = scores - (unit_all.astype(jnp.float32) * unit_price)[None, :]
    best_value, second_value = merged(top_two(values), "mp", keep_two)
    terms = excess_of(values, second_value, is_valid).reshape(dp_count, half)
    owner_terms = lax.all_to_all(terms, "dp", split_axis=0, concat_axis=0, tiled=True)
    highest = jnp.max(owner_terms, axis=0)
    new_prices = own_prices + jnp.maximum(highest, jnp.float32(0.0))
    margin_rows = jnp.where(is_valid, best_value - second_value, jnp.float32(0.0))
    margins = spread_back(ordering, is_valid, margin_rows, unassigned.shape[0])
    bidder_total = lax.psum(jnp.sum(unassigned), "dp")
    return (new_prices, margins, bidder_total)


def solution(mesh):
    return jax.shard_map(
        on_device,
        mesh=mesh,
        in_specs=(P("dp", "mp"), P("dp", "mp"), P("dp"), P("dp")),
        out_specs=(P(("dp", "mp")), P("dp"), P()),
        check_vma=False,
    )
```

profile of v0, /device:TPU:0, one launch (start us, length us, event | category | flops | bytes accessed | tf_op | source)
XLA Modules:
  0.0 91.2 jit_solution(4303682870376259929)
XLA Ops:
  7.2 0.0 all-gather.7.cloned.1.call-start
  7.2 9.2 %all_to_all.28 = bf16[2,80,512]{2,1,0:T(8,128)(2,1)S(1)} all-to-all(bf16[2,80,512]{2,1,0:T(8,128)(2,1)} %bitcast.19), channel_id=1, replica_groups=mesh['dp'=16,'mp'=2] {'mp'}, dimensions={0} | all-to-all | bytes 327680 | tf_op jit(solution)/shard_map/all_to_all | solution.py:68
  16.4 0.7 copy.12
  17.1 0.0 all-gather.7.cloned.1.call-update
  17.1 1.3 %fusion.6 = (s32[]{:T(128)}, s32[160]{0:T(256)S(1)}) fusion(s32[160]{0:T(256)} %param.7), kind=kLoop, calls=%fused_computation.23 | loop fusion | flops 639 | bytes 1284 | tf_op jit(solution)/shard_map/reduce_sum | solution.py:83
  18.4 3.2 %sort.17 = (s32[160]{0:T(256)}, s32[160]{0:T(256)S(1)}) sort(s32[160]{0:T(256)S(1)} %get-tuple-element.35, s32[160]{0:T(256)S(1)} %iota.27), dimensions={0}, to_apply=%region_0.1 | sort | flops 1280 | bytes 2560 | tf_op jit(solution)/shard_map/jit(argsort)/sort | solution.py:41
  21.6 1.6 %gather_fusion = s32[128]{0:T(128)S(1)} fusion(s32[160]{0:T(256)} %param.7, s32[1024]{0:T(1024)S(1)} %pad_clamp_fusion), kind=kCustom, calls=%fused_computation | custom fusion | bytes 1536 | tf_op jit(solution)/shard_map/gather | solution.py:42
  23.3 0.8 gather_fusion.1
  24.1 1.2 %dynamic-slice = u32[1]{0:T(128)} dynamic-slice(u32[32]{0:T(128)} %constant.16, u32[]{:T(128)S(6)} %add.30), dynamic_slice_sizes={1} | dynamic-slice | bytes 12
  26.0 0.9 dynamic-slice_dynamic-update-slice_fusion
  26.9 13.7 %all-reduce.1 = (s32[1280]{0:T(1024)S(1)}, s32[]{:T(128)}) all-reduce(s32[1280]{0:T(1024)S(1)} %dynamic-slice_dynamic-update-slice_fusion, s32[]{:T(128)} %get-tuple-element.34), channel_id=1, replica_groups=mesh['dp'=16,'mp'=2] {'dp'}, use_global_device_ids=true, to_apply=%add | all-reduce | flops 1281 | bytes 10248
  40.6 5.6 %all-gather = bf16[128,1024]{1,0:T(8,128)(2,1)S(1)} all-gather(bf16[128,512]{1,0:T(8,128)(2,1)S(1)} %gather_fusion.1), channel_id=2, replica_groups=mesh['dp'=16,'mp'=2] {'mp'}, dimensions={1}, use_global_device_ids=true | all-gather | bytes 393216 | tf_op jit(solution)/shard_map/all_gather | solution.py:67
  46.3 14.8 %all-gather.7.cloned.1.call-done = bf16[1280,1024]{1,0:T(8,128)(2,1)} async-done(((bf16[80,1024]{1,0:T(8,128)(2,1)}), bf16[1280,1024]{1,0:T(8,128)(2,1)}) %all-gather.7.cloned.1.call-update) | async-done | bytes 2621456 | tf_op jit(solution)/shard_map/all_gather | solution.py:70
  61.0 2.7 %convolution_subtract_fusion = f32[128,1280]{1,0:T(8,128)S(1)} fusion(bf16[128,1024]{1,0:T(8,128)(2,1)S(1)} %all-gather, bf16[1280,1024]{1,0:T(8,128)(2,1)} %all-gather.7.cloned.1.call-done, f32[1280]{0:T(1024)S(1)} %convert_multiply_fusion), kind=kOutput, calls=%fused_computation.2 | convolution fusion | flops 335708160 | bytes 3544064 | tf_op jit(solution)/shard_map/bd,sd->bs/dot_general | solution.py:72
  63.8 0.4 iota_reduce_fusion
  64.2 4.2 %all-gather.3 = f32[2,1,128]{2,1,0:T(1,128)S(1)} all-gather(f32[1,1,128]{2,1,0:T(1,128)S(1)} %bitcast.21), channel_id=3, replica_groups=mesh['dp'=16,'mp'=2] {'mp'}, dimensions={0}, use_global_device_ids=true | all-gather | bytes 1536 | tf_op jit(solution)/shard_map/all_gather | solution.py:11
  68.4 0.2 select_reduce_fusion.1
  68.6 4.2 %all-gather.4 = f32[2,1,128]{2,1,0:T(1,128)S(1)} all-gather(f32[1,1,128]{2,1,0:T(1,128)S(1)} %bitcast.22), channel_id=4, replica_groups=mesh['dp'=16,'mp'=2] {'mp'}, dimensions={0}, use_global_device_ids=true | all-gather | bytes 1536 | tf_op jit(solution)/shard_map/all_gather | solution.py:11
  72.9 0.1 select_reduce_fusion
  73.0 0.7 all_to_all.24
  73.7 3.6 %all-to-all-start.1 = ((f32[16,1,80]{2,1,0:T(1,128)}), f32[16,1,80]{2,1,0:T(1,128)S(1)}, u32[]{:S(2)}, u32[]{:S(2)}) async-start(f32[16,1,80]{2,1,0:T(1,128)} %all_to_all.24), calls=%async_computation.1 | async-start | bytes 16384 | tf_op jit(solution)/shard_map/all_to_all | solution.py:78
  77.3 0.7 select_reduce_fusion.2
  77.9 5.8 %all-to-all-done.1 = f32[16,1,80]{2,1,0:T(1,128)S(1)} async-done(((f32[16,1,80]{2,1,0:T(1,128)}), f32[16,1,80]{2,1,0:T(1,128)S(1)}, u32[]{:S(2)}, u32[]{:S(2)}) %all-to-all-start.1) | async-done | bytes 5152 | tf_op jit(solution)/shard_map/all_to_all | solution.py:78
  83.7 0.6 maximum_add_fusion
  (12 shorter events, 0.1 us)
Async XLA Ops:
  7.2 16.1 %copy-start = (bf16[160,512]{1,0:T(8,128)(2,1)S(1)}, bf16[160,512]{1,0:T(8,128)(2,1)}, u32[]{:S(2)}) copy-start(bf16[160,512]{1,0:T(8,128)(2,1)} %param.4) | copy-start | bytes 491524
  7.2 53.9 %all-gather.7.cloned.1.call-start = ((), (), s32[]{:S(2)}) async-start(), calls=%async_computation.2 | async-start | bytes 2785280 | tf_op jit(solution)/shard_map/all_gather | solution.py:70
  46.2 37.5 %copy-start.1 = (s32[160]{0:T(256)S(1)}, s32[160]{0:T(256)}, u32[]{:S(2)}) copy-start(s32[160]{0:T(256)} %param.6) | copy-start | bytes 1924
  73.7 10.0 %all-to-all-start.1 = ((f32[16,1,80]{2,1,0:T(1,128)}), f32[16,1,80]{2,1,0:T(1,128)S(1)}, u32[]{:S(2)}, u32[]{:S(2)}) async-start(f32[16,1,80]{2,1,0:T(1,128)} %all_to_all.24), calls=%async_computation.1 | async-start | bytes 16384 | tf_op jit(solution)/shard_map/all_to_all | solution.py:78
Sparse Core Ops, SparseCore 0:
  17.2 43.7 all-gather.6
where the time goes:
time: 91.5 us; the launch traced here: 91.2 us
  blocking collectives  37 us (40%)
  waiting for transfers between devices  20.6 us (23%)
  between operations  14.7 us (16%)
  other arithmetic  6.56 us (7%)
  local copies, waits for them, and re-layouts  5.97 us (7%)
  starting transfers between devices  3.59 us (4%)
  matrix products  2.73 us (3%)
    all_gather x1, waiting for transfers between devices, on_device(): slot_rows = lax.all_gather(slot_rows_whole, 'dp', axis=0, tiled=True)  14.8 us
    unnamed x1, blocking collectives  13.7 us
    all_to_all x1, blocking collectives, on_device(): lax.all_to_all(slot_embed, 'mp', split_axis=0, concat_axis=1, tiled=True)  9.2 us
    all_gather x2, blocking collectives, merged(): everything = jax.tree.map(lambda part: lax.all_gather(part, axis), x)  8.47 us
    all_to_all x1, waiting for transfers between devices, on_device(): lax.all_to_all(terms, 'dp', split_axis=0, concat_axis=0, tiled=True)  5.75 us
    all_gather x1, blocking collectives, on_device(): whole_bidders = lax.all_gather(bidders, 'mp', axis=1, tiled=True)  5.62 us
    all_to_all x1, starting transfers between devices, on_device(): lax.all_to_all(terms, 'dp', split_axis=0, concat_axis=0, tiled=True)  3.55 us
    sort x1, other arithmetic, compact(): jnp.argsort(jnp.where(mask > 0, positions, positions + length))[:busy]  3.17 us
  transfers between devices with their start and end apart: 2, of which 2 were waited for; matrix products, arithmetic and copies ran while one was open for 11% of the time, Pallas kernels for 0%

commit v1 on v0

--- a/solution.py
+++ b/solution.py
@@ -67,9 +67,35 @@
     whole_bidders = lax.all_gather(bidders, "mp", axis=1, tiled=True)
     slot_rows_whole = lax.all_to_all(slot_embed, "mp", split_axis=0, concat_axis=1, tiled=True)
     unit_all = jnp.zeros((columns,), jnp.int32)
-    slot_rows = lax.all_gather(slot_rows_whole, "dp", axis=0, tiled=True)
     unit_rows = lax.all_gather(own_units, "dp", axis=0, tiled=True)
-    block = jnp.einsum("bd,sd->bs", whole_bidders, slot_rows, preferred_element_type=jnp.float32)
+
+    def _link_cubes(obj, axis_name, mat):
+        x_new, w1, n_now = (lax.axis_size(axis_name), lax.axis_index(axis_name), obj.shape[0])
+        plain, vec_out = ([], [])
+        low = b_now = obj
+        dev_j = 0
+        while dev_j < x_new // 2 + 1:
+            plain.append(mat(low, (w1 - dev_j) % x_new * n_now))
+            if 0 < dev_j < x_new - x_new // 2:
+                vec_out.append(mat(b_now, (w1 + dev_j) % x_new * n_now))
+            low = lax.ppermute(
+                low, axis_name=axis_name, perm=[(tick, (tick + 1) % x_new) for tick in range(x_new)]
+            )
+            b_now = lax.ppermute(
+                b_now, axis_name, [(tick, (tick - 1) % x_new) for tick in range(x_new)]
+            )
+            dev_j = dev_j + 1
+        all_values = jnp.concatenate([*plain[::-1], *vec_out], axis=1)
+        h_now = jnp.roll(all_values, (w1 - x_new // 2) * plain[0].shape[1], axis=1)
+        return h_now
+
+    block = _link_cubes(
+        slot_rows_whole,
+        "dp",
+        lambda own_block, offset: jnp.einsum(
+            "bd,sd->bs", whole_bidders, own_block, preferred_element_type=jnp.float32
+        ),
+    )
     unit_all = lax.dynamic_update_slice_in_dim(unit_all, unit_rows, jnp.int32(0), 0)
     scores, unit_all = (block, unit_all)
     values = scores - (unit_all.astype(jnp.float32) * unit_price)[None, :]

time: 91.5 us -> 108 us (1.18)
  starting transfers between devices: 3.59 us -> 31.1 us
  between operations: 14.7 us -> 1.71 us
  waiting for transfers between devices: 20.6 us -> 24.5 us
  local copies, waits for them, and re-layouts: 5.97 us -> 4.07 us
    ppermute x0 -> x15, starting transfers between devices: none -> 27.7 us  [the longest x7 27.1 us: _link_cubes(): lax.ppermute(b_now, axis_name, [(tick, (tick - 1) % x_new) for tick in ra...]
    ppermute x0 -> x15, waiting for transfers between devices: none -> 18.8 us  [the longest x8 13.8 us: _link_cubes(): lax.ppermute(low, axis_name=axis_name, perm=[(tick, (tick + 1) % x_new) f...]
    all_gather x1 -> x0, waiting for transfers between devices: 14.8 us -> none  [on_device(): slot_rows = lax.all_gather(slot_rows_whole, 'dp', axis=0, tiled=True)]
    unnamed x7 -> x24, local copies, waits for them, and re-layouts: 2.14 us -> 0.89 us
    dot_general x1 -> x16, matrix products: 2.73 us -> 3.4 us  [on_device(): jnp.einsum('bd,sd->bs', whole_bidders, own_block, preferred_element_type=...]
  transfers between devices with their start and end apart: 2 -> 16, of which waited for: 2 -> 8; matrix products, arithmetic and copies ran while one was open for 11% -> 11% of each run, Pallas kernels for 0% -> 0%
where the time goes in v1:
time: 108 us
  blocking collectives  36.3 us (34%)
  starting transfers between devices  31.1 us (29%)
  waiting for transfers between devices  24.5 us (23%)
  other arithmetic  6.93 us (6%)
  local copies, waits for them, and re-layouts  4.07 us (4%)
  matrix products  3.4 us (3%)
  between operations  1.71 us (2%)
    ppermute x7, starting transfers between devices, _link_cubes(): lax.ppermute(b_now, axis_name, [(tick, (tick - 1) % x_new) for tick in ra...  27.1 us
    ppermute x8, waiting for transfers between devices, _link_cubes(): lax.ppermute(low, axis_name=axis_name, perm=[(tick, (tick + 1) % x_new) f...  13.8 us
    unnamed x1, blocking collectives  13 us
    all_to_all x1, blocking collectives, on_device(): lax.all_to_all(slot_embed, 'mp', split_axis=0, concat_axis=1, tiled=True)  9.2 us
    all_gather x2, blocking collectives, merged(): everything = jax.tree.map(lambda part: lax.all_gather(part, axis), x)  8.46 us
    all_to_all x1, waiting for transfers between devices, on_device(): lax.all_to_all(terms, 'dp', split_axis=0, concat_axis=0, tiled=True)  5.71 us
    all_gather x1, blocking collectives, on_device(): whole_bidders = lax.all_gather(bidders, 'mp', axis=1, tiled=True)  5.62 us
    ppermute x7, waiting for transfers between devices, _link_cubes(): lax.ppermute(b_now, axis_name, [(tick, (tick - 1) % x_new) for tick in ra...  5 us
  transfers between devices with their start and end apart: 16, of which 8 were waited for; matrix products, arithmetic and copies ran while one was open for 11% of the time, Pallas kernels for 0%

profile of v1, /device:TPU:0, one launch (start us, length us, event | category | flops | bytes accessed | tf_op | source)
XLA Modules:
  0.0 108.0 jit_solution(499295315003744248)
XLA Ops:
  0.7 9.2 %all_to_all.28 = bf16[2,80,512]{2,1,0:T(8,128)(2,1)S(1)} all-to-all(bf16[2,80,512]{2,1,0:T(8,128)(2,1)} %bitcast.51), channel_id=1, replica_groups=mesh['dp'=16,'mp'=2] {'mp'}, dimensions={0} | all-to-all | bytes 327680 | tf_op jit(solution)/shard_map/all_to_all | solution.py:68
  10.0 7.4 %collective-permute-done = bf16[80,1024]{1,0:T(8,128)(2,1)S(1)} collective-permute-done((bf16[80,1024]{1,0:T(8,128)(2,1)S(1)}, bf16[80,1024]{1,0:T(8,128)(2,1)S(1)}, u32[]{:S(2)}, u32[]{:S(2)}) %collective-permute-start) | collective-permute-done | bytes 163872 | tf_op jit(solution)/shard_map/ppermute | solution.py:81
  17.4 4.4 %collective-permute-start.8 = (bf16[80,1024]{1,0:T(8,128)(2,1)S(1)}, bf16[80,1024]{1,0:T(8,128)(2,1)S(1)}, u32[]{:S(2)}, u32[]{:S(2)}) collective-permute-start(bf16[80,1024]{1,0:T(8,128)(2,1)S(1)} %bitcast.48), channel_id=1, source_target_pairs={{0,30},{2,0},{4,2},{6,4},{8,6},{10,8},{12,10},{14,12},{16,14},{18,... | collective-permute-start | bytes 491528 | tf_op jit(solution)/shard_map/ppermute | solution.py:84
  21.8 3.0 %collective-permute-done.1 = bf16[80,1024]{1,0:T(8,128)(2,1)S(1)} collective-permute-done((bf16[80,1024]{1,0:T(8,128)(2,1)S(1)}, bf16[80,1024]{1,0:T(8,128)(2,1)S(1)}, u32[]{:S(2)}, u32[]{:S(2)}) %collective-permute-start.1) | collective-permute-done | bytes 163872 | tf_op jit(solution)/shard_map/ppermute | solution.py:81
  24.8 4.5 %collective-permute-start.9 = (bf16[80,1024]{1,0:T(8,128)(2,1)S(1)}, bf16[80,1024]{1,0:T(8,128)(2,1)S(1)}, u32[]{:S(2)}, u32[]{:S(2)}) collective-permute-start(bf16[80,1024]{1,0:T(8,128)(2,1)S(1)} %collective-permute-done.8), channel_id=1, source_target_pairs={{0,30},{2,0},{4,2},{6,4},{8,6},{10,8},{12,10},{14,12},{16,14},{18,... | collective-permute-start | bytes 491528 | tf_op jit(solution)/shard_map/ppermute | solution.py:84
  29.4 2.9 %collective-permute-done.2 = bf16[80,1024]{1,0:T(8,128)(2,1)S(1)} collective-permute-done((bf16[80,1024]{1,0:T(8,128)(2,1)S(1)}, bf16[80,1024]{1,0:T(8,128)(2,1)S(1)}, u32[]{:S(2)}, u32[]{:S(2)}) %collective-permute-start.2) | collective-permute-done | bytes 163872 | tf_op jit(solution)/shard_map/ppermute | solution.py:81
  32.3 1.3 %fusion.6 = (s32[]{:T(128)}, s32[160]{0:T(256)S(1)}) fusion(s32[160]{0:T(256)} %param.7), kind=kLoop, calls=%fused_computation.55 | loop fusion | flops 639 | bytes 1284 | tf_op jit(solution)/shard_map/reduce_sum | solution.py:109
  33.6 3.2 %sort.17 = (s32[160]{0:T(256)}, s32[160]{0:T(256)S(1)}) sort(s32[160]{0:T(256)S(1)} %get-tuple-element.35, s32[160]{0:T(256)S(1)} %iota.27), dimensions={0}, to_apply=%region_0.1 | sort | flops 1280 | bytes 2560 | tf_op jit(solution)/shard_map/jit(argsort)/sort | solution.py:41
  36.8 4.4 %collective-permute-start.10 = (bf16[80,1024]{1,0:T(8,128)(2,1)S(1)}, bf16[80,1024]{1,0:T(8,128)(2,1)S(1)}, u32[]{:S(2)}, u32[]{:S(2)}) collective-permute-start(bf16[80,1024]{1,0:T(8,128)(2,1)S(1)} %collective-permute-done.9), channel_id=1, source_target_pairs={{0,30},{2,0},{4,2},{6,4},{8,6},{10,8},{12,10},{14,12},{16,14},{18,... | collective-permute-start | bytes 491528 | tf_op jit(solution)/shard_map/ppermute | solution.py:84
  41.3 1.6 %gather_fusion = s32[128]{0:T(128)S(1)} fusion(s32[160]{0:T(256)} %param.7, s32[1024]{0:T(1024)S(1)} %pad_clamp_fusion), kind=kCustom, calls=%fused_computation | custom fusion | bytes 1536 | tf_op jit(solution)/shard_map/gather | solution.py:42
  42.9 0.8 gather_fusion.1
  45.0 4.5 %collective-permute-start.11 = (bf16[80,1024]{1,0:T(8,128)(2,1)S(1)}, bf16[80,1024]{1,0:T(8,128)(2,1)S(1)}, u32[]{:S(2)}, u32[]{:S(2)}) collective-permute-start(bf16[80,1024]{1,0:T(8,128)(2,1)S(1)} %collective-permute-done.10), channel_id=1, source_target_pairs={{0,30},{2,0},{4,2},{6,4},{8,6},{10,8},{12,10},{14,12},{16,14},{18,... | collective-permute-start | bytes 491528 | tf_op jit(solution)/shard_map/ppermute | solution.py:84
  49.7 13.0 %all-reduce.1 = (s32[1280]{0:T(1024)S(1)}, s32[]{:T(128)}) all-reduce(s32[1280]{0:T(1024)S(1)} %dynamic-slice_dynamic-update-slice_fusion, s32[]{:T(128)} %get-tuple-element.34), channel_id=1, replica_groups=mesh['dp'=16,'mp'=2] {'dp'}, use_global_device_ids=true, to_apply=%add | all-reduce | flops 1281 | bytes 10248
  62.7 5.6 %all-gather = bf16[128,1024]{1,0:T(8,128)(2,1)S(1)} all-gather(bf16[128,512]{1,0:T(8,128)(2,1)S(1)} %gather_fusion.1), channel_id=2, replica_groups=mesh['dp'=16,'mp'=2] {'mp'}, dimensions={1}, use_global_device_ids=true | all-gather | bytes 393216 | tf_op jit(solution)/shard_map/all_gather | solution.py:67
  68.9 2.3 %collective-permute-done.12 = bf16[80,1024]{1,0:T(8,128)(2,1)S(1)} collective-permute-done((bf16[80,1024]{1,0:T(8,128)(2,1)S(1)}, bf16[80,1024]{1,0:T(8,128)(2,1)S(1)}, u32[]{:S(2)}, u32[]{:S(2)}) %collective-permute-start.12) | collective-permute-done | bytes 163872 | tf_op jit(solution)/shard_map/ppermute | solution.py:84
  71.2 4.6 %collective-permute-start.13 = (bf16[80,1024]{1,0:T(8,128)(2,1)S(1)}, bf16[80,1024]{1,0:T(8,128)(2,1)S(1)}, u32[]{:S(2)}, u32[]{:S(2)}) collective-permute-start(bf16[80,1024]{1,0:T(8,128)(2,1)S(1)} %collective-permute-done.12), channel_id=1, source_target_pairs={{0,30},{2,0},{4,2},{6,4},{8,6},{10,8},{12,10},{14,12},{16,14},{18,... | collective-permute-start | bytes 491528 | tf_op jit(solution)/shard_map/ppermute | solution.py:84
  76.0 2.7 %collective-permute-done.13 = bf16[80,1024]{1,0:T(8,128)(2,1)S(1)} collective-permute-done((bf16[80,1024]{1,0:T(8,128)(2,1)S(1)}, bf16[80,1024]{1,0:T(8,128)(2,1)S(1)}, u32[]{:S(2)}, u32[]{:S(2)}) %collective-permute-start.13) | collective-permute-done | bytes 163872 | tf_op jit(solution)/shard_map/ppermute | solution.py:84
  78.6 4.6 %collective-permute-start.14 = (bf16[80,1024]{1,0:T(8,128)(2,1)S(1)}, bf16[80,1024]{1,0:T(8,128)(2,1)S(1)}, u32[]{:S(2)}, u32[]{:S(2)}) collective-permute-start(bf16[80,1024]{1,0:T(8,128)(2,1)S(1)} %collective-permute-done.13), channel_id=1, source_target_pairs={{0,30},{2,0},{4,2},{6,4},{8,6},{10,8},{12,10},{14,12},{16,14},{18,... | collective-permute-start | bytes 491528 | tf_op jit(solution)/shard_map/ppermute | solution.py:84
  88.0 4.2 %all-gather.4 = f32[2,1,128]{2,1,0:T(1,128)S(1)} all-gather(f32[1,1,128]{2,1,0:T(1,128)S(1)} %bitcast.54), channel_id=4, replica_groups=mesh['dp'=16,'mp'=2] {'mp'}, dimensions={0}, use_global_device_ids=true | all-gather | bytes 1536 | tf_op jit(solution)/shard_map/all_gather | solution.py:11
  92.2 4.2 %all-gather.3 = f32[2,1,128]{2,1,0:T(1,128)S(1)} all-gather(f32[1,1,128]{2,1,0:T(1,128)S(1)} %bitcast.53), channel_id=3, replica_groups=mesh['dp'=16,'mp'=2] {'mp'}, dimensions={0}, use_global_device_ids=true | all-gather | bytes 1536 | tf_op jit(solution)/shard_map/all_gather | solution.py:11
  96.9 0.7 all_to_all.24
  97.5 3.4 %all-to-all-start.1 = ((f32[16,1,80]{2,1,0:T(1,128)}), f32[16,1,80]{2,1,0:T(1,128)S(1)}, u32[]{:S(2)}, u32[]{:S(2)}) async-start(f32[16,1,80]{2,1,0:T(1,128)} %all_to_all.24), calls=%async_computation.1 | async-start | bytes 16384 | tf_op jit(solution)/shard_map/all_to_all | solution.py:104
  101.0 0.7 select_reduce_fusion.2
  101.7 5.7 %all-to-all-done.1 = f32[16,1,80]{2,1,0:T(1,128)S(1)} async-done(((f32[16,1,80]{2,1,0:T(1,128)}), f32[16,1,80]{2,1,0:T(1,128)S(1)}, u32[]{:S(2)}, u32[]{:S(2)}) %all-to-all-start.1) | async-done | bytes 5152 | tf_op jit(solution)/shard_map/all_to_all | solution.py:104
  (72 shorter events, 7.1 us)
Async XLA Ops:
  0.6 42.3 %copy-start = (bf16[160,512]{1,0:T(8,128)(2,1)S(1)}, bf16[160,512]{1,0:T(8,128)(2,1)}, u32[]{:S(2)}) copy-start(bf16[160,512]{1,0:T(8,128)(2,1)} %param.4) | copy-start | bytes 491524
  0.6 43.1 %copy-start.2 = (u32[32]{0:T(128)S(1)}, u32[32]{0:T(128)}, u32[]{:S(2)}) copy-start(u32[32]{0:T(128)} %constant.62) | copy-start | bytes 388
  0.7 48.9 %copy-start.1 = (s32[160]{0:T(256)S(1)}, s32[160]{0:T(256)}, u32[]{:S(2)}) copy-start(s32[160]{0:T(256)} %param.6) | copy-start | bytes 1924
  9.9 7.5 %collective-permute-start = (bf16[80,1024]{1,0:T(8,128)(2,1)S(1)}, bf16[80,1024]{1,0:T(8,128)(2,1)S(1)}, u32[]{:S(2)}, u32[]{:S(2)}) collective-permute-start(bf16[80,1024]{1,0:T(8,128)(2,1)S(1)} %bitcast.47), channel_id=1, source_target_pairs={{0,2},{2,4},{4,6},{6,8},{8,10},{10,12},{12,14},{14,16},{16,18},{18... | collective-permute-start | bytes 491528 | tf_op jit(solution)/shard_map/ppermute | solution.py:81
  17.4 7.5 %collective-permute-start.1 = (bf16[80,1024]{1,0:T(8,128)(2,1)S(1)}, bf16[80,1024]{1,0:T(8,128)(2,1)S(1)}, u32[]{:S(2)}, u32[]{:S(2)}) collective-permute-start(bf16[80,1024]{1,0:T(8,128)(2,1)S(1)} %collective-permute-done), channel_id=1, source_target_pairs={{0,2},{2,4},{4,6},{6,8},{8,10},{10,12},{12,14},{14,16},{16,18},{18... | collective-permute-start | bytes 491528 | tf_op jit(solution)/shard_map/ppermute | solution.py:81
  17.4 7.5 %collective-permute-start.8 = (bf16[80,1024]{1,0:T(8,128)(2,1)S(1)}, bf16[80,1024]{1,0:T(8,128)(2,1)S(1)}, u32[]{:S(2)}, u32[]{:S(2)}) collective-permute-start(bf16[80,1024]{1,0:T(8,128)(2,1)S(1)} %bitcast.48), channel_id=1, source_target_pairs={{0,30},{2,0},{4,2},{6,4},{8,6},{10,8},{12,10},{14,12},{16,14},{18,... | collective-permute-start | bytes 491528 | tf_op jit(solution)/shard_map/ppermute | solution.py:84
  24.8 7.4 %collective-permute-start.2 = (bf16[80,1024]{1,0:T(8,128)(2,1)S(1)}, bf16[80,1024]{1,0:T(8,128)(2,1)S(1)}, u32[]{:S(2)}, u32[]{:S(2)}) collective-permute-start(bf16[80,1024]{1,0:T(8,128)(2,1)S(1)} %collective-permute-done.1), channel_id=1, source_target_pairs={{0,2},{2,4},{4,6},{6,8},{8,10},{10,12},{12,14},{14,16},{16,18},{18... | collective-permute-start | bytes 491528 | tf_op jit(solution)/shard_map/ppermute | solution.py:81
  24.8 11.9 %collective-permute-start.9 = (bf16[80,1024]{1,0:T(8,128)(2,1)S(1)}, bf16[80,1024]{1,0:T(8,128)(2,1)S(1)}, u32[]{:S(2)}, u32[]{:S(2)}) collective-permute-start(bf16[80,1024]{1,0:T(8,128)(2,1)S(1)} %collective-permute-done.8), channel_id=1, source_target_pairs={{0,30},{2,0},{4,2},{6,4},{8,6},{10,8},{12,10},{14,12},{16,14},{18,... | collective-permute-start | bytes 491528 | tf_op jit(solution)/shard_map/ppermute | solution.py:84
  32.3 8.9 %collective-permute-start.3 = (bf16[80,1024]{1,0:T(8,128)(2,1)S(1)}, bf16[80,1024]{1,0:T(8,128)(2,1)S(1)}, u32[]{:S(2)}, u32[]{:S(2)}) collective-permute-start(bf16[80,1024]{1,0:T(8,128)(2,1)S(1)} %collective-permute-done.2), channel_id=1, source_target_pairs={{0,2},{2,4},{4,6},{6,8},{8,10},{10,12},{12,14},{14,16},{16,18},{18... | collective-permute-start | bytes 491528 | tf_op jit(solution)/shard_map/ppermute | solution.py:81
  36.8 8.3 %collective-permute-start.10 = (bf16[80,1024]{1,0:T(8,128)(2,1)S(1)}, bf16[80,1024]{1,0:T(8,128)(2,1)S(1)}, u32[]{:S(2)}, u32[]{:S(2)}) collective-permute-start(bf16[80,1024]{1,0:T(8,128)(2,1)S(1)} %collective-permute-done.9), channel_id=1, source_target_pairs={{0,30},{2,0},{4,2},{6,4},{8,6},{10,8},{12,10},{14,12},{16,14},{18,... | collective-permute-start | bytes 491528 | tf_op jit(solution)/shard_map/ppermute | solution.py:84
  41.2 8.3 %collective-permute-start.4 = (bf16[80,1024]{1,0:T(8,128)(2,1)S(1)}, bf16[80,1024]{1,0:T(8,128)(2,1)S(1)}, u32[]{:S(2)}, u32[]{:S(2)}) collective-permute-start(bf16[80,1024]{1,0:T(8,128)(2,1)S(1)} %collective-permute-done.3), channel_id=1, source_target_pairs={{0,2},{2,4},{4,6},{6,8},{8,10},{10,12},{12,14},{14,16},{16,18},{18... | collective-permute-start | bytes 491528 | tf_op jit(solution)/shard_map/ppermute | solution.py:81
  45.0 23.3 %collective-permute-start.11 = (bf16[80,1024]{1,0:T(8,128)(2,1)S(1)}, bf16[80,1024]{1,0:T(8,128)(2,1)S(1)}, u32[]{:S(2)}, u32[]{:S(2)}) collective-permute-start(bf16[80,1024]{1,0:T(8,128)(2,1)S(1)} %collective-permute-done.10), channel_id=1, source_target_pairs={{0,30},{2,0},{4,2},{6,4},{8,6},{10,8},{12,10},{14,12},{16,14},{18,... | collective-permute-start | bytes 491528 | tf_op jit(solution)/shard_map/ppermute | solution.py:84
  49.5 18.9 %collective-permute-start.5 = (bf16[80,1024]{1,0:T(8,128)(2,1)S(1)}, bf16[80,1024]{1,0:T(8,128)(2,1)S(1)}, u32[]{:S(2)}, u32[]{:S(2)}) collective-permute-start(bf16[80,1024]{1,0:T(8,128)(2,1)S(1)} %collective-permute-done.4), channel_id=1, source_target_pairs={{0,2},{2,4},{4,6},{6,8},{8,10},{10,12},{12,14},{14,16},{16,18},{18... | collective-permute-start | bytes 491528 | tf_op jit(solution)/shard_map/ppermute | solution.py:81
  68.4 2.8 %collective-permute-start.12 = (bf16[80,1024]{1,0:T(8,128)(2,1)S(1)}, bf16[80,1024]{1,0:T(8,128)(2,1)S(1)}, u32[]{:S(2)}, u32[]{:S(2)}) collective-permute-start(bf16[80,1024]{1,0:T(8,128)(2,1)S(1)} %collective-permute-done.11), channel_id=1, source_target_pairs={{0,30},{2,0},{4,2},{6,4},{8,6},{10,8},{12,10},{14,12},{16,14},{18,... | collective-permute-start | bytes 491528 | tf_op jit(solution)/shard_map/ppermute | solution.py:84
  68.4 7.6 %collective-permute-start.6 = (bf16[80,1024]{1,0:T(8,128)(2,1)S(1)}, bf16[80,1024]{1,0:T(8,128)(2,1)S(1)}, u32[]{:S(2)}, u32[]{:S(2)}) collective-permute-start(bf16[80,1024]{1,0:T(8,128)(2,1)S(1)} %collective-permute-done.5), channel_id=1, source_target_pairs={{0,2},{2,4},{4,6},{6,8},{8,10},{10,12},{12,14},{14,16},{16,18},{18... | collective-permute-start | bytes 491528 | tf_op jit(solution)/shard_map/ppermute | solution.py:81
  71.2 7.4 %collective-permute-start.13 = (bf16[80,1024]{1,0:T(8,128)(2,1)S(1)}, bf16[80,1024]{1,0:T(8,128)(2,1)S(1)}, u32[]{:S(2)}, u32[]{:S(2)}) collective-permute-start(bf16[80,1024]{1,0:T(8,128)(2,1)S(1)} %collective-permute-done.12), channel_id=1, source_target_pairs={{0,30},{2,0},{4,2},{6,4},{8,6},{10,8},{12,10},{14,12},{16,14},{18,... | collective-permute-start | bytes 491528 | tf_op jit(solution)/shard_map/ppermute | solution.py:84
  76.0 7.5 %collective-permute-start.7 = (bf16[80,1024]{1,0:T(8,128)(2,1)S(1)}, bf16[80,1024]{1,0:T(8,128)(2,1)S(1)}, u32[]{:S(2)}, u32[]{:S(2)}) collective-permute-start(bf16[80,1024]{1,0:T(8,128)(2,1)S(1)} %collective-permute-done.6), channel_id=1, source_target_pairs={{0,2},{2,4},{4,6},{6,8},{8,10},{10,12},{12,14},{14,16},{16,18},{18... | collective-permute-start | bytes 491528 | tf_op jit(solution)/shard_map/ppermute | solution.py:81
  78.6 8.2 %collective-permute-start.14 = (bf16[80,1024]{1,0:T(8,128)(2,1)S(1)}, bf16[80,1024]{1,0:T(8,128)(2,1)S(1)}, u32[]{:S(2)}, u32[]{:S(2)}) collective-permute-start(bf16[80,1024]{1,0:T(8,128)(2,1)S(1)} %collective-permute-done.13), channel_id=1, source_target_pairs={{0,30},{2,0},{4,2},{6,4},{8,6},{10,8},{12,10},{14,12},{16,14},{18,... | collective-permute-start | bytes 491528 | tf_op jit(solution)/shard_map/ppermute | solution.py:84
  97.5 9.8 %all-to-all-start.1 = ((f32[16,1,80]{2,1,0:T(1,128)}), f32[16,1,80]{2,1,0:T(1,128)S(1)}, u32[]{:S(2)}, u32[]{:S(2)}) async-start(f32[16,1,80]{2,1,0:T(1,128)} %all_to_all.24), calls=%async_computation.1 | async-start | bytes 16384 | tf_op jit(solution)/shard_map/all_to_all | solution.py:104
